TPU v7x, 32 devices: a whole 2x2x4 slice. The times are simulated.
32 devices in a mesh: seq: 16 (over z, y, x), tp: 2 (over core).
Axes of the slice: x: 2, y: 2, z: 4, core: 2. Of those that a mesh axis runs over, the one named last changes fastest.
Arguments:
- img: bfloat16 [4, 512, 3072], P(None, 'seq', 'tp'), may hold values from -6 to 6
- txt: bfloat16 [4, 64, 3072], P(None, 'seq', 'tp'), may hold values from -6 to 6
- prev_mod: bfloat16 [4, 512, 3072], P(None, 'seq', 'tp'), may hold values from -47 to 47
- cache: float32 [4, 512, 3072], P(None, 'seq', 'tp'), may hold values from -6 to 6
- modulation: bfloat16 [3, 4, 3072], P(None, None, 'tp'), may hold values from -4 to 4
- w_qkv: bfloat16 [3072, 3, 2048], P('seq', None, 'tp'), may hold values from -1 to 1, as said below
- qk_gain: float32 [2, 2048], P(None, 'tp'), may hold values from 0.5 to 6, as said below
- output_weight: bfloat16 [2048, 3072], P('tp'), may hold values from -0.1875 to 0.1875
- text_len: int32 [4], replicated, may hold values from 1 to 64
- refresh: int32 [4], replicated, may hold values from 0 to 1, as said below
Outputs:
- out_img: float32 [4, 512, 3072], P(None, 'seq', 'tp')
- new_cache: float32 [4, 512, 3072], P(None, 'seq', 'tp')
- rel_l1: float32 [4], replicated
Inputs may be any that keep to these rules, and one draw needn't show every extreme that they name: `refresh`: at least one sequence has flag 1 and at least one has flag 0. `w_qkv`: entries of spread about one over the square root of 3072. `qk_gain`: positive.
All inputs are finite; a program needn't handle non-finite values.
Results may differ from a plain program's by a relative error of at most 0.013.
The roundings to bfloat16 on the way count: a program that leaves them out, or rounds other values in their place, can miss the bound.
Values may be sent and summed in bfloat16 or wider, within the bound.
A program may use at most 128 MiB of HBM per device.

v0:
```python
import jax
import jax.numpy as jnp
from jax import lax
from jax.sharding import PartitionSpec as P

HD = 128
EPS = 0.1
NEG = -1e30


def unit_heads(block, gain):
    shaped = block.reshape(block.shape[:-1] + (block.shape[-1] // HD, HD))
    scaled = shaped * lax.rsqrt(jnp.mean(jnp.square(shaped), axis=-1, keepdims=True) + EPS)
    return scaled.reshape(block.shape) * gain


def local(img, txt, prev_mod, cache, modulation, w_qkv, qk_gain, output_weight, text_len, refresh):
    batch, img_rows, width_loc = img.shape
    txt_rows = txt.shape[1]
    rows = txt_rows + img_rows
    joined = jnp.concatenate([txt, img], axis=1)
    local_mods = modulation.astype(jnp.float32)
    wide, wide_mod = (
        lax.all_gather(joined, "tp", axis=2, tiled=True),
        lax.all_gather(modulation, "tp", axis=2, tiled=True),
    )
    wide_mods = wide_mod.astype(jnp.float32)
    values = wide.astype(jnp.float32)
    center = jnp.mean(values, axis=2, keepdims=True)
    spread = jnp.mean(jnp.square(values - center), axis=2, keepdims=True)
    normed = (values - center) * lax.rsqrt(spread + EPS)
    modded = (normed * (1.0 + wide_mods[1][:, None, :]) + wide_mods[0][:, None, :]).astype(
        jnp.bfloat16
    )
    offset = lax.axis_index("tp") * width_loc
    own_image = lax.dynamic_slice_in_dim(modded[:, txt_rows:, :], offset, width_loc, 2)
    previous = prev_mod.astype(jnp.float32)
    gap = jnp.sum(jnp.abs(own_image.astype(jnp.float32) - previous), axis=(1, 2))
    base_sum = jnp.sum(jnp.abs(previous), axis=(1, 2))
    numer, denom = lax.psum((gap, base_sum), ("seq", "tp"))
    rel_l1 = numer / jnp.maximum(denom, 1.0)
    columns = w_qkv.shape[2]
    projected = jnp.einsum(
        "btd,dkc->btkc",
        modded,
        lax.all_gather(w_qkv, "seq", axis=0, tiled=True),
        preferred_element_type=jnp.float32,
    )
    heads = columns // HD
    query = unit_heads(projected[:, txt_rows:, 0, :], qk_gain[0]).astype(jnp.bfloat16)
    query_heads = query.reshape(batch, img_rows, heads, HD)
    keyed = unit_heads(projected[:, :, 1, :], qk_gain[1]).astype(jnp.bfloat16)
    valued = projected[:, :, 2, :].astype(jnp.bfloat16)
    paired = jnp.stack([keyed, valued], axis=2)
    score_scale = 1.0 / HD**0.5
    start_top = jnp.full((batch, heads, img_rows), NEG, jnp.float32)
    piece = lax.all_gather(paired, "seq", axis=1, tiled=True)
    top = start_top
    count = piece.shape[1]
    index = jnp.arange(count, dtype=jnp.int32)
    slot = index % rows
    text_pos = index // rows * txt_rows + slot
    valid = (slot >= txt_rows)[None, :] | (text_pos[None, :] < text_len[:, None])
    keys = piece[:, :, 0, :].reshape(batch, count, heads, HD)
    vals = piece[:, :, 1, :].reshape(batch, count, heads, HD)
    logit_scores = (
        jnp.einsum("bqhc,bkhc->bhqk", query_heads, keys, preferred_element_type=jnp.float32)
        * score_scale
    )
    logit_scores = jnp.where(valid[:, None, None, :], logit_scores, NEG)
    new_top = jnp.maximum(top, jnp.max(logit_scores, axis=3))
    attention_weights = jnp.where(
        valid[:, None, None, :], jnp.exp(logit_scores - new_top[..., None]), 0.0
    )
    total = jnp.sum(attention_weights, axis=3)
    summed_output = jnp.einsum(
        "bhqk,bkhc->bhqc",
        attention_weights.astype(jnp.bfloat16),
        vals,
        preferred_element_type=jnp.float32,
    )
    top, total, summed_output = (new_top, total, summed_output)
    attended_values = (summed_output / total[..., None]).astype(jnp.bfloat16)
    attended_values = attended_values.transpose(0, 2, 1, 3).reshape(batch, img_rows, columns)
    partial_output = jnp.einsum(
        "pxr,ro->pxo", attended_values, output_weight, preferred_element_type=jnp.float32
    )
    whole = lax.psum(partial_output.astype(jnp.bfloat16), "tp").astype(jnp.float32)
    mixed_heads = lax.dynamic_slice_in_dim(whole, lax.axis_index("tp") * width_loc, width_loc, 2)
    resid = local_mods[2][:, None, :] * mixed_heads
    flag = (refresh == 1)[:, None, None]
    new_cache = jnp.where(flag, resid, cache)
    out_img = img.astype(jnp.float32) + new_cache
    return (out_img, new_cache, rel_l1)


def solution(mesh):
    return jax.shard_map(
        local,
        mesh=mesh,
        in_specs=(
            P(None, "seq", "tp"),
            P(None, "seq", "tp"),
            P(None, "seq", "tp"),
            P(None, "seq", "tp"),
            P(None, None, "tp"),
            P("seq", None, "tp"),
            P(None, "tp"),
            P("tp", None),
            P(),
            P(),
        ),
        out_specs=(P(None, "seq", "tp"), P(None, "seq", "tp"), P()),
        check_vma=False,
    )
```

profile of v0, /device:TPU:0, one launch (start us, length us, event | category | flops | bytes accessed | tf_op | source)
XLA Modules:
  0.0 434.7 jit_solution(10169232465015273428)
XLA Ops:
  7.2 0.0 all-gather.3.cloned.1.call-start
  7.2 0.7 all-gather.3.cloned.1.call-update
  7.9 0.0 copy-start.3
  7.9 0.0 all-gather.5.cloned.1.call-start
  8.0 2.2 all_gather.13
  10.2 1.1 pad_maximum_fusion.1
  11.3 2.5 all_gather.12
  13.8 0.2 convert_reduce_fusion
  14.1 0.4 fusion.14
  14.5 0.0 copy-done.3
  14.5 0.5 fusion.17
  15.0 209.3 %all-gather.3.cloned.1.call-done = bf16[3072,3,1024]{2,0,1:T(8,128)(2,1)} async-done(((bf16[192,3,1024]{2,0,1:T(8,128)(2,1)}), bf16[3072,3,1024]{2,0,1:T(8,128)(2,1)}) %all-gather.3.cloned.1.call-update) | async-done | bytes 18874384 | tf_op jit(solution)/shard_map/all_gather | solution.py:46
  224.3 8.1 %fusion = f32[4,36,3,1024]{3,1,2,0:T(8,128)S(1)} fusion(bf16[3072,3,1024]{2,0,1:T(8,128)(2,1)} %all-gather.3.cloned.1.call-done, bf16[4,36,3072]{2,1,0:T(8,128)(2,1)S(1)} %fusion.17), kind=kOutput, calls=%fused_computation | convolution fusion | flops 2717908992 | bytes 21528576 | tf_op jit(solution)/shard_map/btd,dkc->btkc/dot_general | solution.py:43
  232.4 0.9 slice_multiply_fusion
  233.3 0.8 slice.62
  234.1 1.2 reshape.130
  235.3 0.9 reduce_sum.66
  236.1 1.0 copy.47
  237.1 0.1 copy.48
  237.2 1.0 mul.103
  238.3 1.3 mul.104
  239.5 0.4 fusion.51
  239.9 0.0 copy-start.2
  239.9 0.0 copy-start.4
  239.9 1.1 pad_maximum_fusion
  241.0 1.3 copy.50
  242.3 0.0 all-gather.5.cloned.1.call-update
  242.3 0.0 all-reduce.3.cloned.1.call-start
  242.4 1.1 slice.53
  243.5 0.0 copy-done.2
  243.5 1.3 fusion.49
  244.8 40.5 %all-reduce = (f32[4]{0:T(128)S(1)}, f32[4]{0:T(128)S(1)}) all-reduce(f32[4]{0:T(128)S(1)} %get-tuple-element.4, f32[4]{0:T(128)S(1)} %get-tuple-element.3), channel_id=1, replica_groups=mesh['seq'=16,'tp'=2] {'seq','tp'}, use_global_device_ids=true, to_apply=%region_8.9 | all-reduce | flops 8 | bytes 64 | tf_op jit(solution)/shard_map/psum | solution.py:40
  285.3 0.0 copy-done.4
  285.3 0.1 compare_or_fusion
  285.4 0.1 slice.48
  285.5 0.1 copy.66
  285.6 0.2 fusion.52
  285.8 0.2 fusion.54
  286.0 77.3 %all-gather.5.cloned.1.call-done = bf16[4,576,2,1024]{3,0,2,1:T(4,128)(2,1)} async-done(((bf16[4,36,2,1024]{3,0,2,1:T(4,128)(2,1)}), bf16[4,576,2,1024]{3,0,2,1:T(4,128)(2,1)}) %all-gather.5.cloned.1.call-update) | async-done | bytes 9437200 | tf_op jit(solution)/shard_map/all_gather | solution.py:57
  363.3 10.7 %fusion.70 = (bf16[4,576,1,1024]{3,0,2,1:T(4,128)(2,1)}, bf16[4,576,1,1024]{3,0,2,1:T(4,128)(2,1)}) fusion(bf16[4,576,2,1024]{3,0,2,1:T(4,128)(2,1)} %all-gather.5.cloned.1.call-done), kind=kLoop, calls=%fused_computation.82 | loop fusion | bytes 18874368 | tf_op jit(solution)/shard_map/slice | solution.py:64
  374.0 8.0 %reshape.131 = bf16[4,576,8,128]{3,2,0,1:T(8,128)(2,1)} reshape(bf16[4,576,1,1024]{3,0,2,1:T(4,128)(2,1)} %get-tuple-element.9) | data formatting | bytes 9437184 | tf_op jit(solution)/shard_map/reshape;squeeze | solution.py:64
  382.0 7.5 %fusion.13 = (f32[4,8,32]{2,1,0:T(8,128)S(1)}, f32[4,8,32,576]{3,2,1,0:T(8,128)S(1)}) fusion(pred[4,576]{1,0:T(4,128)(4,1)S(1)} %compare_or_fusion, bf16[4,576,8,128]{3,2,0,1:T(8,128)(2,1)} %reshape.131, bf16[4,32,8,128]{3,2,1,0:T(8,128)(2,1)S(1)} %fusion.54), kind=kOutput, calls=%fused_computation.15 | convolution fusion | flops 152763392 | bytes 7346432 | tf_op jit(solution)/shard_map/bqhc,bkhc->bhqk/dot_general | solution.py:67
  389.5 8.0 %reshape.132 = bf16[4,576,8,128]{3,2,0,1:T(8,128)(2,1)} reshape(bf16[4,576,1,1024]{3,0,2,1:T(4,128)(2,1)} %get-tuple-element.10) | data formatting | bytes 9437184 | tf_op jit(solution)/shard_map/reshape;squeeze | solution.py:65
  397.6 0.0 slice-start
  397.6 0.8 fusion.18
  398.4 0.0 slice-start.1
  398.4 8.1 %fusion.41 = bf16[4,8,4,8,128]{4,3,2,1,0:T(8,128)(2,1)S(1)} fusion(bf16[4,576,8,128]{3,2,0,1:T(8,128)(2,1)} %reshape.132, f32[4,8,32,576]{3,2,1,0:T(8,128)S(1)} %get-tuple-element.16, f32[4,8,32]{2,1,0:T(8,128)S(1)} %broadcast_maximum_fusion, pred[4,576]{1,0:T(4,128)(4,1)S(1)} %compare_or_fusion, f32[4,32,8]{1,2,0:T(8,128)S(1)} %bitcast.67), kind=kOutput, calls=%fused_computation.30 | convolution fusion | flops 154206208 | bytes 7350528 | tf_op jit(solution)/shard_map/bhqk,bkhc->bhqc/dot_general | solution.py:76
  406.5 0.0 slice-done
  406.5 0.0 slice-done.1
  406.5 0.0 copy-start.5
  406.5 0.0 copy-start
  406.6 0.0 copy-start.1
  406.6 1.9 fusion.8
  408.4 0.0 all-reduce.3.cloned.1.call-update
  408.5 0.0 copy-done.5
  408.5 0.5 maximum_divide_fusion
  409.0 0.7 bitcast_convert_fusion
  409.7 16.1 %all-reduce.3.cloned.1.call-done = bf16[4,32,3072]{2,1,0:T(8,128)(2,1)} async-done(((bf16[4,32,3072]{2,1,0:T(8,128)(2,1)}), bf16[4,32,3072]{2,1,0:T(8,128)(2,1)}) %all-reduce.3.cloned.1.call-update) | async-done | bytes 786448 | tf_op jit(solution)/shard_map/psum | solution.py:88
  425.8 0.0 copy-done
  425.8 0.0 copy-done.1
  425.8 2.4 convert_add_fusion
  (12 shorter events, 0.1 us)
Async XLA Ops:
  7.2 217.1 %all-gather.3.cloned.1.call-start = ((), (), s32[]{:S(2)}) async-start(), calls=%async_computation | async-start | bytes 20054016 | tf_op jit(solution)/shard_map/all_gather | solution.py:46
  7.9 6.6 %copy-start.3 = (f32[2,1024]{1,0:T(2,128)S(1)}, f32[2,1024]{1,0:T(2,128)}, u32[]{:S(2)}) copy-start(f32[2,1024]{1,0:T(2,128)} %param.16) | copy-start | bytes 24580
  7.9 355.4 %all-gather.5.cloned.1.call-start = ((), (), s32[]{:S(2)}) async-start(), calls=%async_computation.1 | async-start | bytes 10027008 | tf_op jit(solution)/shard_map/all_gather | solution.py:57
  239.9 3.6 copy-start.2
  239.9 45.4 %copy-start.4 = (s32[4]{0:T(128)S(1)}, s32[4]{0:T(128)}, u32[]{:S(2)}) copy-start(s32[4]{0:T(128)} %param.18) | copy-start | bytes 52
  242.3 183.5 %all-reduce.3.cloned.1.call-start = ((), (), s32[]{:S(2)}) async-start(), calls=%async_computation.2 | async-start | bytes 1572864 | tf_op jit(solution)/shard_map/psum | solution.py:88
  397.6 8.9 %slice-start = ((s8[6291456]{0:T(1024)(128)(4,1)}), s8[4194304]{0:T(1024)(128)(4,1)S(1)}, s32[]{:S(2)}) async-start(s8[6291456]{0:T(1024)(128)(4,1)} %bitcast.62), calls=%async_computation.3 | async-start | bytes 8388608
  398.4 8.1 %slice-start.1 = ((s8[6291456]{0:T(1024)(128)(4,1)}), s8[2097152]{0:T(1024)(128)(4,1)S(1)}, s32[]{:S(2)}) async-start(s8[6291456]{0:T(1024)(128)(4,1)} %bitcast.62), calls=%async_computation.4 | async-start | bytes 4194304
  406.5 1.9 copy-start.5
  406.5 19.2 %copy-start = (bf16[4,32,1536]{2,1,0:T(8,128)(2,1)S(1)}, bf16[4,32,1536]{2,1,0:T(8,128)(2,1)}, u32[]{:S(2)}) copy-start(bf16[4,32,1536]{2,1,0:T(8,128)(2,1)} %param.10) | copy-start | bytes 1179652
  406.6 19.2 %copy-start.1 = (f32[4,32,1536]{2,1,0:T(8,128)S(1)}, f32[4,32,1536]{2,1,0:T(8,128)}, u32[]{:S(2)}) copy-start(f32[4,32,1536]{2,1,0:T(8,128)} %param.13) | copy-start | bytes 2359300
Sparse Core Ops, SparseCore 0:
  10.6 213.6 all-gather.2
  242.4 120.8 all-gather.4
  408.6 17.1 all-reduce.2
where the time goes:
time: 436 us; the launch traced here: 435 us
  waiting for transfers between devices  303 us (69%)
  blocking collectives  45.3 us (10%)
  local copies, waits for them, and re-layouts  34.7 us (8%)
  matrix products  25.6 us (6%)
  between operations  14 us (3%)
  other arithmetic  11.8 us (3%)
    all_gather x1, waiting for transfers between devices, local(): lax.all_gather(w_qkv, 'seq', axis=0, tiled=True)  209 us
    all_gather x1, waiting for transfers between devices, local(): piece = lax.all_gather(paired, 'seq', axis=1, tiled=True)  77.3 us
    psum x1, blocking collectives, local(): numer, denom = lax.psum((gap, base_sum), ('seq', 'tp'))  40.5 us
    psum x1, waiting for transfers between devices, local(): lax.psum(partial_output.astype(jnp.bfloat16), 'tp').astype(jnp.float32)  16.1 us
    slice x1, local copies, waits for them, and re-layouts, local(): keys = piece[:, :, 0, :].reshape(batch, count, heads, HD)  10.7 us
  transfers between devices with their start and end apart: 3, of which 3 were waited for; matrix products, arithmetic and copies ran while one was open for 2% of the time, Pallas kernels for 0%

commit v1 on v0

--- a/solution.py
+++ b/solution.py
@@ -15,6 +15,19 @@
 
 
 def local(img, txt, prev_mod, cache, modulation, w_qkv, qk_gain, output_weight, text_len, refresh):
+
+    def _proceed_members_all(content):
+        world_n = lax.axis_size("seq")
+        series = [(j0, (j0 + 1) % world_n) for j0 in range(world_n)]
+        piece_next = [None] * world_n
+        piece_next[world_n - 1] = content
+        for pp in range(world_n - 2, -1, -1):
+            piece_next[pp] = lax.ppermute(piece_next[pp + 1], "seq", perm=series)
+        formed = jnp.concatenate(piece_next, 1)
+        row_out = lax.axis_index("seq")
+        main = jnp.roll(formed, (row_out + 1) * content.shape[1], 1)
+        return main
+
     batch, img_rows, width_loc = img.shape
     txt_rows = txt.shape[1]
     rows = txt_rows + img_rows
@@ -54,7 +67,7 @@
     paired = jnp.stack([keyed, valued], axis=2)
     score_scale = 1.0 / HD**0.5
     start_top = jnp.full((batch, heads, img_rows), NEG, jnp.float32)
-    piece = lax.all_gather(paired, "seq", axis=1, tiled=True)
+    piece = _proceed_members_all(paired)
     top = start_top
     count = piece.shape[1]
     index = jnp.arange(count, dtype=jnp.int32)

time: 436 us -> 709 us (1.63)
  local copies, waits for them, and re-layouts: 34.7 us -> 176 us
  waiting for transfers between devices: 303 us -> 438 us
  matrix products: 25.6 us -> 13.5 us
    ppermute x0 -> x15, waiting for transfers between devices: none -> 210 us  [_proceed_members_all(): piece_next[pp] = lax.ppermute(piece_next[pp + 1], 'seq', perm=series)]
    concatenate x0 -> x1, local copies, waits for them, and re-layouts: none -> 134 us  [_proceed_members_all(): main = jnp.roll(formed, (row_out + 1) * content.shape[1], 1)]
    all_gather x1 -> x0, waiting for transfers between devices: 77.3 us -> none  [local(): piece = lax.all_gather(paired, 'seq', axis=1, tiled=True)]
    ppermute x0 -> x15, local copies, waits for them, and re-layouts: none -> 16.5 us  [_proceed_members_all(): piece_next[pp] = lax.ppermute(piece_next[pp + 1], 'seq', perm=series)]
    another operation x2 -> x0, local copies, waits for them, and re-layouts: 16.1 us -> none  [the longest x1 8.05 us: local(): vals = piece[:, :, 1, :].reshape(batch, count, heads, HD)]
    unnamed x17 -> x73, local copies, waits for them, and re-layouts: 0.14 us -> 13 us
  transfers between devices with their start and end apart: 3 -> 17, of which waited for: 3 -> 16; matrix products, arithmetic and copies ran while one was open for 2% -> 3% of each run, Pallas kernels for 0% -> 0%
where the time goes in v1:
time: 709 us; the launch traced here: 703 us
  waiting for transfers between devices  438 us (62%)
  local copies, waits for them, and re-layouts  176 us (25%)
  blocking collectives  44.7 us (6%)
  between operations  14.5 us (2%)
  matrix products  13.5 us (2%)
  other arithmetic  11.9 us (2%)
    ppermute x15, waiting for transfers between devices, _proceed_members_all(): piece_next[pp] = lax.ppermute(piece_next[pp + 1], 'seq', perm=series)  210 us
    all_gather x1, waiting for transfers between devices, local(): lax.all_gather(w_qkv, 'seq', axis=0, tiled=True)  209 us
    concatenate x1, local copies, waits for them, and re-layouts, _proceed_members_all(): main = jnp.roll(formed, (row_out + 1) * content.shape[1], 1)  134 us
    psum x1, blocking collectives, local(): numer, denom = lax.psum((gap, base_sum), ('seq', 'tp'))  40 us
    psum x1, waiting for transfers between devices, local(): lax.psum(partial_output.astype(jnp.bfloat16), 'tp').astype(jnp.float32)  17.6 us
    ppermute x15, local copies, waits for them, and re-layouts, _proceed_members_all(): piece_next[pp] = lax.ppermute(piece_next[pp + 1], 'seq', perm=series)  16.5 us
  transfers between devices with their start and end apart: 17, of which 16 were waited for; matrix products, arithmetic and copies ran while one was open for 3% of the time, Pallas kernels for 0%

profile of v1, /device:TPU:0, one launch (start us, length us, event | category | flops | bytes accessed | tf_op | source)
XLA Modules:
  0.0 703.1 jit_solution(5250217931778651678)
XLA Ops:
  8.0 2.2 all_gather.10
  10.2 1.1 pad_maximum_fusion.1
  11.3 2.5 all_gather.9
  15.0 209.3 %all-gather.2.cloned.1.call-done = bf16[3072,3,1024]{2,0,1:T(8,128)(2,1)} async-done(((bf16[192,3,1024]{2,0,1:T(8,128)(2,1)}), bf16[3072,3,1024]{2,0,1:T(8,128)(2,1)}) %all-gather.2.cloned.1.call-update) | async-done | bytes 18874384 | tf_op jit(solution)/shard_map/all_gather | solution.py:59
  224.3 8.1 %fusion = f32[4,36,3,1024]{3,1,2,0:T(8,128)S(1)} fusion(bf16[3072,3,1024]{2,0,1:T(8,128)(2,1)} %all-gather.2.cloned.1.call-done, bf16[4,36,3072]{2,1,0:T(8,128)(2,1)S(1)} %fusion.17), kind=kOutput, calls=%fused_computation | convolution fusion | flops 2717908992 | bytes 21528576 | tf_op jit(solution)/shard_map/btd,dkc->btkc/dot_general | solution.py:56
  232.4 0.8 slice.60
  233.2 0.9 slice_multiply_fusion
  234.1 1.2 reshape.130
  235.3 0.9 reduce_sum.66
  236.1 1.0 copy.98
  237.2 1.0 mul.106
  238.3 1.3 mul.107
  239.9 1.0 pad_maximum_fusion
  241.0 0.8 copy-done
  242.3 1.5 collective-permute-start
  243.8 16.5 %collective-permute-done = bf16[4,36,2,1024]{3,0,2,1:T(4,128)(2,1)S(1)} collective-permute-done((bf16[4,36,2,1024]{3,0,2,1:T(4,128)(2,1)S(1)}, bf16[4,36,2,1024]{3,0,2,1:T(4,128)(2,1)S(1)}, u32[]{:S(2)}, u32[]{:S(2)}) %collective-permute-start) | collective-permute-done | bytes 589856 | tf_op jit(solution)/shard_map/ppermute | solution.py:25
  260.3 0.9 copy-done.4
  261.1 17.1 %collective-permute-done.1 = bf16[4,36,2,1024]{3,0,2,1:T(4,128)(2,1)S(1)} collective-permute-done((bf16[4,36,2,1024]{3,0,2,1:T(4,128)(2,1)S(1)}, bf16[4,36,2,1024]{3,0,2,1:T(4,128)(2,1)S(1)}, u32[]{:S(2)}, u32[]{:S(2)}) %collective-permute-start.1) | collective-permute-done | bytes 589856 | tf_op jit(solution)/shard_map/ppermute | solution.py:25
  278.2 0.8 copy-done.6
  279.0 16.2 %collective-permute-done.2 = bf16[4,36,2,1024]{3,0,2,1:T(4,128)(2,1)S(1)} collective-permute-done((bf16[4,36,2,1024]{3,0,2,1:T(4,128)(2,1)S(1)}, bf16[4,36,2,1024]{3,0,2,1:T(4,128)(2,1)S(1)}, u32[]{:S(2)}, u32[]{:S(2)}) %collective-permute-start.2) | collective-permute-done | bytes 589856 | tf_op jit(solution)/shard_map/ppermute | solution.py:25
  295.3 0.8 copy-done.8
  296.1 15.4 %collective-permute-done.3 = bf16[4,36,2,1024]{3,0,2,1:T(4,128)(2,1)S(1)} collective-permute-done((bf16[4,36,2,1024]{3,0,2,1:T(4,128)(2,1)S(1)}, bf16[4,36,2,1024]{3,0,2,1:T(4,128)(2,1)S(1)}, u32[]{:S(2)}, u32[]{:S(2)}) %collective-permute-start.3) | collective-permute-done | bytes 589856 | tf_op jit(solution)/shard_map/ppermute | solution.py:25
  311.5 0.8 copy-done.10
  312.3 14.5 %collective-permute-done.4 = bf16[4,36,2,1024]{3,0,2,1:T(4,128)(2,1)S(1)} collective-permute-done((bf16[4,36,2,1024]{3,0,2,1:T(4,128)(2,1)S(1)}, bf16[4,36,2,1024]{3,0,2,1:T(4,128)(2,1)S(1)}, u32[]{:S(2)}, u32[]{:S(2)}) %collective-permute-start.4) | collective-permute-done | bytes 589856 | tf_op jit(solution)/shard_map/ppermute | solution.py:25
  326.8 0.8 copy-done.12
  327.6 13.7 %collective-permute-done.5 = bf16[4,36,2,1024]{3,0,2,1:T(4,128)(2,1)S(1)} collective-permute-done((bf16[4,36,2,1024]{3,0,2,1:T(4,128)(2,1)S(1)}, bf16[4,36,2,1024]{3,0,2,1:T(4,128)(2,1)S(1)}, u32[]{:S(2)}, u32[]{:S(2)}) %collective-permute-start.5) | collective-permute-done | bytes 589856 | tf_op jit(solution)/shard_map/ppermute | solution.py:25
  341.3 0.8 copy-done.14
  342.2 13.6 %collective-permute-done.6 = bf16[4,36,2,1024]{3,0,2,1:T(4,128)(2,1)S(1)} collective-permute-done((bf16[4,36,2,1024]{3,0,2,1:T(4,128)(2,1)S(1)}, bf16[4,36,2,1024]{3,0,2,1:T(4,128)(2,1)S(1)}, u32[]{:S(2)}, u32[]{:S(2)}) %collective-permute-start.6) | collective-permute-done | bytes 589856 | tf_op jit(solution)/shard_map/ppermute | solution.py:25
  355.8 0.8 copy-done.16
  356.6 14.8 %collective-permute-done.7 = bf16[4,36,2,1024]{3,0,2,1:T(4,128)(2,1)S(1)} collective-permute-done((bf16[4,36,2,1024]{3,0,2,1:T(4,128)(2,1)S(1)}, bf16[4,36,2,1024]{3,0,2,1:T(4,128)(2,1)S(1)}, u32[]{:S(2)}, u32[]{:S(2)}) %collective-permute-start.7) | collective-permute-done | bytes 589856 | tf_op jit(solution)/shard_map/ppermute | solution.py:25
  371.4 0.8 copy-done.18
  372.2 15.9 %collective-permute-done.8 = bf16[4,36,2,1024]{3,0,2,1:T(4,128)(2,1)S(1)} collective-permute-done((bf16[4,36,2,1024]{3,0,2,1:T(4,128)(2,1)S(1)}, bf16[4,36,2,1024]{3,0,2,1:T(4,128)(2,1)S(1)}, u32[]{:S(2)}, u32[]{:S(2)}) %collective-permute-start.8) | collective-permute-done | bytes 589856 | tf_op jit(solution)/shard_map/ppermute | solution.py:25
  388.1 0.8 copy-done.20
  389.0 17.1 %collective-permute-done.9 = bf16[4,36,2,1024]{3,0,2,1:T(4,128)(2,1)S(1)} collective-permute-done((bf16[4,36,2,1024]{3,0,2,1:T(4,128)(2,1)S(1)}, bf16[4,36,2,1024]{3,0,2,1:T(4,128)(2,1)S(1)}, u32[]{:S(2)}, u32[]{:S(2)}) %collective-permute-start.9) | collective-permute-done | bytes 589856 | tf_op jit(solution)/shard_map/ppermute | solution.py:25
  406.0 0.8 copy-done.22
  406.9 18.2 %collective-permute-done.10 = bf16[4,36,2,1024]{3,0,2,1:T(4,128)(2,1)S(1)} collective-permute-done((bf16[4,36,2,1024]{3,0,2,1:T(4,128)(2,1)S(1)}, bf16[4,36,2,1024]{3,0,2,1:T(4,128)(2,1)S(1)}, u32[]{:S(2)}, u32[]{:S(2)}) %collective-permute-start.10) | collective-permute-done | bytes 589856 | tf_op jit(solution)/shard_map/ppermute | solution.py:25
  425.1 0.8 copy-done.24
  425.9 19.4 %collective-permute-done.11 = bf16[4,36,2,1024]{3,0,2,1:T(4,128)(2,1)S(1)} collective-permute-done((bf16[4,36,2,1024]{3,0,2,1:T(4,128)(2,1)S(1)}, bf16[4,36,2,1024]{3,0,2,1:T(4,128)(2,1)S(1)}, u32[]{:S(2)}, u32[]{:S(2)}) %collective-permute-start.11) | collective-permute-done | bytes 589856 | tf_op jit(solution)/shard_map/ppermute | solution.py:25
  445.3 1.1 slice.51
  446.4 17.7 %collective-permute-done.12 = bf16[4,36,2,1024]{3,0,2,1:T(4,128)(2,1)} collective-permute-done((bf16[4,36,2,1024]{3,0,2,1:T(4,128)(2,1)S(1)}, bf16[4,36,2,1024]{3,0,2,1:T(4,128)(2,1)}, u32[]{:S(2)}, u32[]{:S(2)}) %collective-permute-start.12) | collective-permute-done | bytes 589856 | tf_op jit(solution)/shard_map/ppermute | solution.py:25
  464.2 1.4 fusion.49
  465.6 40.0 %all-reduce = (f32[4]{0:T(128)}, f32[4]{0:T(128)}) all-reduce(f32[4]{0:T(128)S(1)} %get-tuple-element.4, f32[4]{0:T(128)S(1)} %get-tuple-element.3), channel_id=1, replica_groups=mesh['seq'=16,'tp'=2] {'seq','tp'}, use_global_device_ids=true, to_apply=%region_8.9 | all-reduce | flops 8 | bytes 64 | tf_op jit(solution)/shard_map/psum | solution.py:53
  505.9 2.5 collective-permute-start.14
  510.3 1.2 copy.112
  511.5 1.2 copy.111
  512.7 1.2 copy.110
  513.9 1.2 copy.109
  515.1 1.2 copy.108
  516.3 1.2 copy.107
  517.4 1.2 copy.106
  518.7 1.2 copy.105
  519.8 2.3 copy.104
  522.1 2.2 copy.103
  524.5 1.2 copy.102
  525.6 133.6 %concatenate.10 = bf16[4,1152,2,1024]{3,1,2,0:T(8,128)(2,1)} concatenate(bf16[4,36,2,1024]{3,1,2,0:T(8,128)(2,1)} %copy.102, bf16[4,36,2,1024]{3,1,2,0:T(8,128)(2,1)} %copy.103, bf16[4,36,2,1024]{3,1,2,0:T(8,128)(2,1)} %copy.104, bf16[4,36,2,1024]{3,1,2,0:T(8,128)(2,1)} %copy.105, bf16[4,36,2,1024]{3,1,2,0:T(8,128)(2,1)} %copy.106, bf16[4,36,2,1024]{3,1,2,0:T(8,128)(2,1)} %copy.107, ...), dimensions={1} | concatenate | bytes 37748736 | tf_op jit(solution)/shard_map/jit(_roll_dynamic)/concatenate | solution.py:28
  659.2 6.5 constant_dynamic-slice_fusion
  665.8 1.2 copy.142
  667.0 1.7 fusion.13
  668.7 1.2 copy.143
  670.0 0.8 fusion.18
  670.8 1.8 fusion.41
  673.1 1.9 fusion.8
  676.2 17.6 %all-reduce.3.cloned.1.call-done = bf16[4,32,3072]{2,1,0:T(8,128)(2,1)} async-done(((bf16[4,32,3072]{2,1,0:T(8,128)(2,1)}), bf16[4,32,3072]{2,1,0:T(8,128)(2,1)}) %all-reduce.3.cloned.1.call-update) | async-done | bytes 786448 | tf_op jit(solution)/shard_map/psum | solution.py:101
  693.8 2.4 convert_add_fusion
  (106 shorter events, 6.8 us)
Async XLA Ops:
  7.2 217.1 %all-gather.2.cloned.1.call-start = ((), (), s32[]{:S(2)}) async-start(), calls=%async_computation | async-start | bytes 20054016 | tf_op jit(solution)/shard_map/all_gather | solution.py:59
  7.9 6.6 copy-start.28
  7.9 685.9 %all-reduce.3.cloned.1.call-start = ((), (), s32[]{:S(2)}) async-start(), calls=%async_computation.1 | async-start | bytes 1572864 | tf_op jit(solution)/shard_map/psum | solution.py:101
  239.9 265.7 %copy-start.29 = (s32[4]{0:T(128)S(1)}, s32[4]{0:T(128)}, u32[]{:S(2)}) copy-start(s32[4]{0:T(128)} %param.18) | copy-start | bytes 52
  241.0 0.8 copy-start
  242.3 18.0 %collective-permute-start = (bf16[4,36,2,1024]{3,0,2,1:T(4,128)(2,1)S(1)}, bf16[4,36,2,1024]{3,0,2,1:T(4,128)(2,1)S(1)}, u32[]{:S(2)}, u32[]{:S(2)}) collective-permute-start(bf16[4,36,2,1024]{3,0,2,1:T(4,128)(2,1)S(1)} %copy.101), channel_id=1, source_target_pairs={{0,2},{2,4},{4,6},{6,8},{8,10},{10,12},{12,14},{14,16},{16,18},{18... | collective-permute-start | bytes 1769480 | tf_op jit(solution)/shard_map/ppermute | solution.py:25
  260.3 0.9 copy-start.4
  261.1 17.1 %collective-permute-start.1 = (bf16[4,36,2,1024]{3,0,2,1:T(4,128)(2,1)S(1)}, bf16[4,36,2,1024]{3,0,2,1:T(4,128)(2,1)S(1)}, u32[]{:S(2)}, u32[]{:S(2)}) collective-permute-start(bf16[4,36,2,1024]{3,0,2,1:T(4,128)(2,1)S(1)} %collective-permute-done), channel_id=1, source_target_pairs={{0,2},{2,4},{4,6},{6,8},{8,10},{10,12},{12,14},{14,16},{16,18},{18... | collective-permute-start | bytes 1769480 | tf_op jit(solution)/shard_map/ppermute | solution.py:25
  278.2 0.8 copy-start.6
  279.0 16.2 %collective-permute-start.2 = (bf16[4,36,2,1024]{3,0,2,1:T(4,128)(2,1)S(1)}, bf16[4,36,2,1024]{3,0,2,1:T(4,128)(2,1)S(1)}, u32[]{:S(2)}, u32[]{:S(2)}) collective-permute-start(bf16[4,36,2,1024]{3,0,2,1:T(4,128)(2,1)S(1)} %collective-permute-done.1), channel_id=1, source_target_pairs={{0,2},{2,4},{4,6},{6,8},{8,10},{10,12},{12,14},{14,16},{16,18},{18... | collective-permute-start | bytes 1769480 | tf_op jit(solution)/shard_map/ppermute | solution.py:25
  295.3 0.8 copy-start.8
  296.1 15.4 %collective-permute-start.3 = (bf16[4,36,2,1024]{3,0,2,1:T(4,128)(2,1)S(1)}, bf16[4,36,2,1024]{3,0,2,1:T(4,128)(2,1)S(1)}, u32[]{:S(2)}, u32[]{:S(2)}) collective-permute-start(bf16[4,36,2,1024]{3,0,2,1:T(4,128)(2,1)S(1)} %collective-permute-done.2), channel_id=1, source_target_pairs={{0,2},{2,4},{4,6},{6,8},{8,10},{10,12},{12,14},{14,16},{16,18},{18... | collective-permute-start | bytes 1769480 | tf_op jit(solution)/shard_map/ppermute | solution.py:25
  311.5 0.8 copy-start.10
  312.3 14.5 %collective-permute-start.4 = (bf16[4,36,2,1024]{3,0,2,1:T(4,128)(2,1)S(1)}, bf16[4,36,2,1024]{3,0,2,1:T(4,128)(2,1)S(1)}, u32[]{:S(2)}, u32[]{:S(2)}) collective-permute-start(bf16[4,36,2,1024]{3,0,2,1:T(4,128)(2,1)S(1)} %collective-permute-done.3), channel_id=1, source_target_pairs={{0,2},{2,4},{4,6},{6,8},{8,10},{10,12},{12,14},{14,16},{16,18},{18... | collective-permute-start | bytes 1769480 | tf_op jit(solution)/shard_map/ppermute | solution.py:25
  326.8 0.8 copy-start.12
  327.6 13.7 %collective-permute-start.5 = (bf16[4,36,2,1024]{3,0,2,1:T(4,128)(2,1)S(1)}, bf16[4,36,2,1024]{3,0,2,1:T(4,128)(2,1)S(1)}, u32[]{:S(2)}, u32[]{:S(2)}) collective-permute-start(bf16[4,36,2,1024]{3,0,2,1:T(4,128)(2,1)S(1)} %collective-permute-done.4), channel_id=1, source_target_pairs={{0,2},{2,4},{4,6},{6,8},{8,10},{10,12},{12,14},{14,16},{16,18},{18... | collective-permute-start | bytes 1769480 | tf_op jit(solution)/shard_map/ppermute | solution.py:25
  341.3 0.9 copy-start.14
  342.1 13.6 %collective-permute-start.6 = (bf16[4,36,2,1024]{3,0,2,1:T(4,128)(2,1)S(1)}, bf16[4,36,2,1024]{3,0,2,1:T(4,128)(2,1)S(1)}, u32[]{:S(2)}, u32[]{:S(2)}) collective-permute-start(bf16[4,36,2,1024]{3,0,2,1:T(4,128)(2,1)S(1)} %collective-permute-done.5), channel_id=1, source_target_pairs={{0,2},{2,4},{4,6},{6,8},{8,10},{10,12},{12,14},{14,16},{16,18},{18... | collective-permute-start | bytes 1769480 | tf_op jit(solution)/shard_map/ppermute | solution.py:25
  355.8 0.8 copy-start.16
  356.6 14.8 %collective-permute-start.7 = (bf16[4,36,2,1024]{3,0,2,1:T(4,128)(2,1)S(1)}, bf16[4,36,2,1024]{3,0,2,1:T(4,128)(2,1)S(1)}, u32[]{:S(2)}, u32[]{:S(2)}) collective-permute-start(bf16[4,36,2,1024]{3,0,2,1:T(4,128)(2,1)S(1)} %collective-permute-done.6), channel_id=1, source_target_pairs={{0,2},{2,4},{4,6},{6,8},{8,10},{10,12},{12,14},{14,16},{16,18},{18... | collective-permute-start | bytes 1769480 | tf_op jit(solution)/shard_map/ppermute | solution.py:25
  371.4 0.8 copy-start.18
  372.2 15.9 %collective-permute-start.8 = (bf16[4,36,2,1024]{3,0,2,1:T(4,128)(2,1)S(1)}, bf16[4,36,2,1024]{3,0,2,1:T(4,128)(2,1)S(1)}, u32[]{:S(2)}, u32[]{:S(2)}) collective-permute-start(bf16[4,36,2,1024]{3,0,2,1:T(4,128)(2,1)S(1)} %collective-permute-done.7), channel_id=1, source_target_pairs={{0,2},{2,4},{4,6},{6,8},{8,10},{10,12},{12,14},{14,16},{16,18},{18... | collective-permute-start | bytes 1769480 | tf_op jit(solution)/shard_map/ppermute | solution.py:25
  388.1 0.8 copy-start.20
  389.0 17.1 %collective-permute-start.9 = (bf16[4,36,2,1024]{3,0,2,1:T(4,128)(2,1)S(1)}, bf16[4,36,2,1024]{3,0,2,1:T(4,128)(2,1)S(1)}, u32[]{:S(2)}, u32[]{:S(2)}) collective-permute-start(bf16[4,36,2,1024]{3,0,2,1:T(4,128)(2,1)S(1)} %collective-permute-done.8), channel_id=1, source_target_pairs={{0,2},{2,4},{4,6},{6,8},{8,10},{10,12},{12,14},{14,16},{16,18},{18... | collective-permute-start | bytes 1769480 | tf_op jit(solution)/shard_map/ppermute | solution.py:25
  406.0 0.8 copy-start.22
  406.9 18.2 %collective-permute-start.10 = (bf16[4,36,2,1024]{3,0,2,1:T(4,128)(2,1)S(1)}, bf16[4,36,2,1024]{3,0,2,1:T(4,128)(2,1)S(1)}, u32[]{:S(2)}, u32[]{:S(2)}) collective-permute-start(bf16[4,36,2,1024]{3,0,2,1:T(4,128)(2,1)S(1)} %collective-permute-done.9), channel_id=1, source_target_pairs={{0,2},{2,4},{4,6},{6,8},{8,10},{10,12},{12,14},{14,16},{16,18},{18... | collective-permute-start | bytes 1769480 | tf_op jit(solution)/shard_map/ppermute | solution.py:25
  425.1 0.8 copy-start.24
  425.9 19.4 %collective-permute-start.11 = (bf16[4,36,2,1024]{3,0,2,1:T(4,128)(2,1)S(1)}, bf16[4,36,2,1024]{3,0,2,1:T(4,128)(2,1)S(1)}, u32[]{:S(2)}, u32[]{:S(2)}) collective-permute-start(bf16[4,36,2,1024]{3,0,2,1:T(4,128)(2,1)S(1)} %collective-permute-done.10), channel_id=1, source_target_pairs={{0,2},{2,4},{4,6},{6,8},{8,10},{10,12},{12,14},{14,16},{16,18},{18... | collective-permute-start | bytes 1769480 | tf_op jit(solution)/shard_map/ppermute | solution.py:25
  445.3 18.9 %copy-start.26 = (bf16[4,36,2,1024]{3,0,2,1:T(4,128)(2,1)}, bf16[4,36,2,1024]{3,0,2,1:T(4,128)(2,1)S(1)}, u32[]{:S(2)}) copy-start(bf16[4,36,2,1024]{3,0,2,1:T(4,128)(2,1)S(1)} %collective-permute-done.11) | copy-start | bytes 1769476
  445.3 18.9 %collective-permute-start.12 = (bf16[4,36,2,1024]{3,0,2,1:T(4,128)(2,1)S(1)}, bf16[4,36,2,1024]{3,0,2,1:T(4,128)(2,1)}, u32[]{:S(2)}, u32[]{:S(2)}) collective-permute-start(bf16[4,36,2,1024]{3,0,2,1:T(4,128)(2,1)S(1)} %collective-permute-done.11), channel_id=1, source_target_pairs={{0,2},{2,4},{4,6},{6,8},{8,10},{10,12},{12,14},{14,16},{16,18},{18... | collective-permute-start | bytes 1769480 | tf_op jit(solution)/shard_map/ppermute | solution.py:25
  446.4 62.4 %copy-start.5 = (bf16[4,36,2,1024]{3,0,2,1:T(4,128)(2,1)S(1)}, bf16[4,36,2,1024]{3,0,2,1:T(4,128)(2,1)}, u32[]{:S(2)}) copy-start(bf16[4,36,2,1024]{3,0,2,1:T(4,128)(2,1)} %copy-done.4) | copy-start | bytes 1769476
  464.2 41.7 %collective-permute-start.13 = (bf16[4,36,2,1024]{3,0,2,1:T(4,128)(2,1)}, bf16[4,36,2,1024]{3,0,2,1:T(4,128)(2,1)}, u32[]{:S(2)}, u32[]{:S(2)}) collective-permute-start(bf16[4,36,2,1024]{3,0,2,1:T(4,128)(2,1)} %collective-permute-done.12), channel_id=1, source_target_pairs={{0,2},{2,4},{4,6},{6,8},{8,10},{10,12},{12,14},{14,16},{16,18},{18... | collective-permute-start | bytes 1769480 | tf_op jit(solution)/shard_map/ppermute | solution.py:25
  465.6 43.6 %copy-start.7 = (bf16[4,36,2,1024]{3,0,2,1:T(4,128)(2,1)S(1)}, bf16[4,36,2,1024]{3,0,2,1:T(4,128)(2,1)}, u32[]{:S(2)}) copy-start(bf16[4,36,2,1024]{3,0,2,1:T(4,128)(2,1)} %copy-done.6) | copy-start | bytes 1769476
  505.8 3.8 copy-start.9
  505.9 18.6 %collective-permute-start.14 = (bf16[4,36,2,1024]{3,0,2,1:T(4,128)(2,1)}, bf16[4,36,2,1024]{3,0,2,1:T(4,128)(2,1)S(1)}, u32[]{:S(2)}, u32[]{:S(2)}) collective-permute-start(bf16[4,36,2,1024]{3,0,2,1:T(4,128)(2,1)} %collective-permute-done.13), channel_id=1, source_target_pairs={{0,2},{2,4},{4,6},{6,8},{8,10},{10,12},{12,14},{14,16},{16,18},{18... | collective-permute-start | bytes 1769480 | tf_op jit(solution)/shard_map/ppermute | solution.py:25
  508.4 1.5 copy-start.11
  508.9 1.4 copy-start.13
  509.2 2.3 copy-start.15
  509.6 3.1 copy-start.17
  509.9 3.9 copy-start.19
  510.3 4.7 copy-start.21
  511.5 4.7 copy-start.23
  512.7 4.8 copy-start.25
  513.9 4.8 copy-start.27
  518.7 7.0 copy-start.1
  669.9 2.7 slice-start
  670.8 2.2 slice-start.1
  673.0 1.9 copy-start.30
  673.0 1.9 copy-start.31
  673.0 2.0 copy-start.32
  673.0 20.8 %copy-start.2 = (bf16[4,32,1536]{2,1,0:T(8,128)(2,1)S(1)}, bf16[4,32,1536]{2,1,0:T(8,128)(2,1)}, u32[]{:S(2)}) copy-start(bf16[4,32,1536]{2,1,0:T(8,128)(2,1)} %param.10) | copy-start | bytes 1179652
  673.0 20.8 %copy-start.3 = (f32[4,32,1536]{2,1,0:T(8,128)S(1)}, f32[4,32,1536]{2,1,0:T(8,128)}, u32[]{:S(2)}) copy-start(f32[4,32,1536]{2,1,0:T(8,128)} %param.13) | copy-start | bytes 2359300
Sparse Core Ops, SparseCore 0:
  10.6 213.6 all-gather.1
  675.1 18.6 all-reduce.2
